TPU v7x, 256 devices: a whole 4x4x8 slice. The times are simulated.
256 devices in a mesh: fsdp: 16 (over y, z_lo, core), sp: 16 (over x, z_hi).
Axes of the slice: x: 4, y: 4, z: 8 (z_hi: 4, z_lo: 2; z = z_hi * 2 + z_lo), core: 2. Of those that a mesh axis runs over, the one named last changes fastest.
Arguments:
- hidden: bfloat16 [16, 4096, 5120], P('fsdp', 'sp'), may hold values from -6 to 6
- queries: bfloat16 [16, 4096, 4096], P('fsdp', 'sp'), may hold values from -240 to 240
- norm_gain: float32 [5120], replicated, may hold values from 0.5 to 1.5
- kv_weight: bfloat16 [5120, 2048], P('fsdp'), may hold values from -0.078125 to 0.078125
- value_bias: float32 [1024], replicated, may hold values from -3 to 3
- doc_lengths: int32 [16, 16], P('fsdp'), may hold values from 1 to 1024, 4096 in all within a row
Outputs:
- attended: bfloat16 [16, 4096, 4096], P('fsdp', 'sp')
Inputs may be any that keep to these rules, and one draw needn't show every extreme that they name: `doc_lengths`: each row sums to 4096 and its largest entry is 1024.
All inputs are finite; a program needn't handle non-finite values.
Results may differ from a plain program's by a relative error of at most 0.0067.
Values may be sent and summed in bfloat16 or wider, within the bound.
A program may use at most 128 MiB of HBM per device.

v0:
```python
import jax
import jax.numpy as jnp
from jax import lax
from jax.sharding import PartitionSpec as P

QH = 32
KVH = 8
HD = 128
EPS = 1e-06


def from_behind(value, axis, by):
    count = lax.axis_size(axis)
    pairs = [(i, i + by) for i in range(count) if 0 <= i + by < count]
    return lax.ppermute(value, axis, pairs)


def attend_near(query_rows, key_all, value_all, query_pos, key_pos, query_ids, key_ids):
    token_count = query_rows.shape[0]
    ratio = QH // KVH
    scale = HD ** (-0.5)
    allowed = (
        (key_pos[None, :] >= 0)
        & (key_pos[None, :] <= query_pos[:, None])
        & (key_ids[None, :] == query_ids[:, None])
    )
    query_groups = jnp.transpose(query_rows.reshape(token_count, KVH, ratio, HD), (1, 0, 2, 3))
    key_groups = jnp.transpose(key_all, (1, 0, 2))
    value_groups = jnp.transpose(value_all, (1, 0, 2))

    def one_group(operands):
        query_one, key_one, value_one = operands
        scores = (
            jnp.einsum("qrd,kd->rqk", query_one, key_one, preferred_element_type=jnp.float32)
            * scale
        )
        scores = jnp.where(allowed[None], scores, -jnp.inf)
        highest = jnp.max(scores, axis=-1, keepdims=True)
        probs = jnp.exp(scores - highest)
        probs = (probs / jnp.sum(probs, axis=-1, keepdims=True)).astype(jnp.bfloat16)
        output = jnp.einsum("rqk,kd->qrd", probs, value_one, preferred_element_type=jnp.float32)
        return output.astype(jnp.bfloat16)

    outputs = lax.map(one_group, (query_groups, key_groups, value_groups))
    return jnp.transpose(outputs, (1, 0, 2, 3)).reshape(token_count, QH * HD)


def shards(hidden, queries, norm_gain, kv_weight, value_bias, doc_lengths):
    token_count = hidden.shape[1]
    group_size = lax.axis_size("sp")
    query_rows = queries[0]
    wide = hidden[0].astype(jnp.float32)
    normed = (
        wide * lax.rsqrt(jnp.mean(wide * wide, axis=-1, keepdims=True) + EPS) * norm_gain
    ).astype(jnp.bfloat16)
    projected = jnp.dot(
        normed,
        lax.all_gather(kv_weight, "fsdp", axis=0, tiled=True),
        preferred_element_type=jnp.float32,
    )
    keys = projected[:, : KVH * HD].astype(jnp.bfloat16).reshape(token_count, KVH, HD)
    values = (
        (projected[:, KVH * HD :] + value_bias).astype(jnp.bfloat16).reshape(token_count, KVH, HD)
    )
    ends = jnp.cumsum(doc_lengths[0])
    reach = group_size // 4
    first = lax.axis_index("sp") * token_count
    key_parts = [keys]
    value_parts = [values]
    for back in range(1, reach + 1):
        key_far, value_far = from_behind((keys, values), "sp", back)
        key_parts.insert(0, key_far)
        value_parts.insert(0, value_far)
    key_all = jnp.concatenate(key_parts, axis=0)
    value_all = jnp.concatenate(value_parts, axis=0)
    query_pos = first + jnp.arange(token_count, dtype=jnp.int32)
    key_pos = first - reach * token_count + jnp.arange(key_all.shape[0], dtype=jnp.int32)
    query_ids = jnp.sum((query_pos[:, None] >= ends[None, :]).astype(jnp.int32), axis=1)
    key_ids = jnp.sum((key_pos[:, None] >= ends[None, :]).astype(jnp.int32), axis=1)
    result = attend_near(query_rows, key_all, value_all, query_pos, key_pos, query_ids, key_ids)
    return result.reshape(1, token_count, QH * HD)


def solution(mesh):
    in_specs = (
        P("fsdp", "sp", None),
        P("fsdp", "sp", None),
        P(),
        P("fsdp", None),
        P(),
        P("fsdp", None),
    )
    out_specs = P("fsdp", "sp", None)
    return jax.shard_map(shards, mesh=mesh, in_specs=in_specs, out_specs=out_specs, check_vma=False)
```

profile of v0, /device:TPU:135, one launch (start us, length us, event | category | flops | bytes accessed | tf_op | source)
XLA Modules:
  0.0 336.2 jit_solution(246101491837138390)
XLA Ops:
  10.7 114.0 %all-gather.2.cloned.1.call-done = bf16[5120,2048]{1,0:T(8,128)(2,1)} async-done(((bf16[320,2048]{1,0:T(8,128)(2,1)}), bf16[5120,2048]{1,0:T(8,128)(2,1)}) %all-gather.2.cloned.1.call-update) | async-done | bytes 20971536 | tf_op jit(solution)/shard_map/all_gather | solution.py:58
  124.7 9.9 %fusion.53 = f32[256,2048]{1,0:T(8,128)S(1)} fusion(bf16[5120,2048]{1,0:T(8,128)(2,1)} %all-gather.2.cloned.1.call-done, bf16[1,256,5120]{2,1,0:T(8,128)(2,1)S(1)} %copy-done, f32[5120]{0:T(1024)S(1)} %copy-done.6, f32[256]{0:T(256)S(1)} %add_rsqrt_fusion), kind=kOutput, calls=%fused_computation.37 | convolution fusion | flops 5373952000 | bytes 25711616 | tf_op jit(solution)/shard_map/dot_general | solution.py:56
  140.4 4.1 %copy.46 = bf16[1,256,4096]{1,2,0:T(8,128)(2,1)} copy(bf16[1,256,4096]{2,1,0:T(8,128)(2,1)} %param.9) | data formatting | bytes 4194304 | tf_op args[1]
  148.3 5.8 %collective-permute-done = bf16[256,8,128]{0,2,1:T(8,128)(2,1)} collective-permute-done((bf16[256,8,128]{0,2,1:T(8,128)(2,1)S(1)}, bf16[256,8,128]{0,2,1:T(8,128)(2,1)}, u32[]{:S(2)}, u32[]{:S(2)}) %collective-permute-start) | collective-permute-done | bytes 524320 | tf_op jit(solution)/shard_map/ppermute | solution.py:15
  156.4 35.8 %collective-permute-done.1 = bf16[256,8,128]{0,2,1:T(8,128)(2,1)} collective-permute-done((bf16[256,8,128]{0,2,1:T(8,128)(2,1)S(1)}, bf16[256,8,128]{0,2,1:T(8,128)(2,1)}, u32[]{:S(2)}, u32[]{:S(2)}) %collective-permute-start.1) | collective-permute-done | bytes 524320 | tf_op jit(solution)/shard_map/ppermute | solution.py:15
  194.6 32.9 %collective-permute-start.7 = (bf16[256,8,128]{2,0,1:T(8,128)(2,1)S(1)}, bf16[256,8,128]{2,0,1:T(8,128)(2,1)S(1)}, u32[]{:S(2)}, u32[]{:S(2)}) collective-permute-start(bf16[256,8,128]{2,0,1:T(8,128)(2,1)S(1)} %copy_bitcast_fusion), channel_id=1, source_target_pairs={{0,1},{1,2},{2,3},{3,4},{4,5},{5,6},{6,7},{7,8},{8,9},{9,10},{10,1... | collective-permute-start | bytes 1572872 | tf_op jit(solution)/shard_map/ppermute | solution.py:15
  228.9 6.2 %collective-permute-done.6 = bf16[256,8,128]{2,0,1:T(8,128)(2,1)S(1)} collective-permute-done((bf16[256,8,128]{2,0,1:T(8,128)(2,1)S(1)}, bf16[256,8,128]{2,0,1:T(8,128)(2,1)S(1)}, u32[]{:S(2)}, u32[]{:S(2)}) %collective-permute-start.6) | collective-permute-done | bytes 524320 | tf_op jit(solution)/shard_map/ppermute | solution.py:15
  235.2 23.7 %collective-permute-done.7 = bf16[256,8,128]{2,0,1:T(8,128)(2,1)S(1)} collective-permute-done((bf16[256,8,128]{2,0,1:T(8,128)(2,1)S(1)}, bf16[256,8,128]{2,0,1:T(8,128)(2,1)S(1)}, u32[]{:S(2)}, u32[]{:S(2)}) %collective-permute-start.7) | collective-permute-done | bytes 524320 | tf_op jit(solution)/shard_map/ppermute | solution.py:15
  260.6 64.7 %while.11 = (s32[]{:T(128)}, bf16[8,256,4,128]{1,3,2,0:T(8,128)(2,1)}, bf16[8,1280,128]{1,2,0:T(8,128)(2,1)}, bf16[8,1280,128]{2,1,0:T(8,128)(2,1)}, bf16[8,256,...) while((s32[]{:T(128)}, ...), condition=%wide.region_7.8_spmd.clone, body=%wide.region_4.7_spmd.clone.sunk | while | flops 1019874816 | bytes 2777453 | solution.py:44
  261.6 2.9 exponential_reduce_fusion.2
  264.5 4.2 %fusion.78 = bf16[8,256,4,128]{1,3,2,0:T(8,128)(2,1)} fusion(bf16[8,256,4,128]{1,3,2,0:T(8,128)(2,1)} %get-tuple-element.178, s32[]{:T(128)} %get-tuple-element.177, f32[4,256]{1,0:T(4,128)S(1)} %exponential_reduce_fusion.2, bf16[8,1280,128]{1,2,0:T(8,128)(2,1)} %get-tuple-element.190, pred[256,1280]{0,1:T(8,128)(4,1)S(1)} %compare_and_fusion.2, ...), kind=kOutput, calls=%fused_computation.10.clone.1 | convolution fusion | flops 677775616 | bytes 1513472 | tf_op jit(solution)/shard_map/while/body/eval_jaxpr/rqk,kd->qrd/dot_general | solution.py:41
  269.7 2.9 exponential_reduce_fusion.2
  272.6 4.1 %fusion.78 = bf16[8,256,4,128]{1,3,2,0:T(8,128)(2,1)} fusion(bf16[8,256,4,128]{1,3,2,0:T(8,128)(2,1)} %get-tuple-element.178, s32[]{:T(128)} %get-tuple-element.177, f32[4,256]{1,0:T(4,128)S(1)} %exponential_reduce_fusion.2, bf16[8,1280,128]{1,2,0:T(8,128)(2,1)} %get-tuple-element.190, pred[256,1280]{0,1:T(8,128)(4,1)S(1)} %compare_and_fusion.2, ...), kind=kOutput, calls=%fused_computation.10.clone.1 | convolution fusion | flops 677775616 | bytes 1513472 | tf_op jit(solution)/shard_map/while/body/eval_jaxpr/rqk,kd->qrd/dot_general | solution.py:41
  280.6 4.1 %fusion.78 = bf16[8,256,4,128]{1,3,2,0:T(8,128)(2,1)} fusion(bf16[8,256,4,128]{1,3,2,0:T(8,128)(2,1)} %get-tuple-element.178, s32[]{:T(128)} %get-tuple-element.177, f32[4,256]{1,0:T(4,128)S(1)} %exponential_reduce_fusion.2, bf16[8,1280,128]{1,2,0:T(8,128)(2,1)} %get-tuple-element.190, pred[256,1280]{0,1:T(8,128)(4,1)S(1)} %compare_and_fusion.2, ...), kind=kOutput, calls=%fused_computation.10.clone.1 | convolution fusion | flops 677775616 | bytes 1513472 | tf_op jit(solution)/shard_map/while/body/eval_jaxpr/rqk,kd->qrd/dot_general | solution.py:41
  285.8 2.9 exponential_reduce_fusion.2
  288.7 4.2 %fusion.78 = bf16[8,256,4,128]{1,3,2,0:T(8,128)(2,1)} fusion(bf16[8,256,4,128]{1,3,2,0:T(8,128)(2,1)} %get-tuple-element.178, s32[]{:T(128)} %get-tuple-element.177, f32[4,256]{1,0:T(4,128)S(1)} %exponential_reduce_fusion.2, bf16[8,1280,128]{1,2,0:T(8,128)(2,1)} %get-tuple-element.190, pred[256,1280]{0,1:T(8,128)(4,1)S(1)} %compare_and_fusion.2, ...), kind=kOutput, calls=%fused_computation.10.clone.1 | convolution fusion | flops 677775616 | bytes 1513472 | tf_op jit(solution)/shard_map/while/body/eval_jaxpr/rqk,kd->qrd/dot_general | solution.py:41
  293.9 2.9 exponential_reduce_fusion.2
  296.8 4.2 %fusion.78 = bf16[8,256,4,128]{1,3,2,0:T(8,128)(2,1)} fusion(bf16[8,256,4,128]{1,3,2,0:T(8,128)(2,1)} %get-tuple-element.178, s32[]{:T(128)} %get-tuple-element.177, f32[4,256]{1,0:T(4,128)S(1)} %exponential_reduce_fusion.2, bf16[8,1280,128]{1,2,0:T(8,128)(2,1)} %get-tuple-element.190, pred[256,1280]{0,1:T(8,128)(4,1)S(1)} %compare_and_fusion.2, ...), kind=kOutput, calls=%fused_computation.10.clone.1 | convolution fusion | flops 677775616 | bytes 1513472 | tf_op jit(solution)/shard_map/while/body/eval_jaxpr/rqk,kd->qrd/dot_general | solution.py:41
  302.0 2.9 exponential_reduce_fusion.2
  304.9 4.2 %fusion.78 = bf16[8,256,4,128]{1,3,2,0:T(8,128)(2,1)} fusion(bf16[8,256,4,128]{1,3,2,0:T(8,128)(2,1)} %get-tuple-element.178, s32[]{:T(128)} %get-tuple-element.177, f32[4,256]{1,0:T(4,128)S(1)} %exponential_reduce_fusion.2, bf16[8,1280,128]{1,2,0:T(8,128)(2,1)} %get-tuple-element.190, pred[256,1280]{0,1:T(8,128)(4,1)S(1)} %compare_and_fusion.2, ...), kind=kOutput, calls=%fused_computation.10.clone.1 | convolution fusion | flops 677775616 | bytes 1513472 | tf_op jit(solution)/shard_map/while/body/eval_jaxpr/rqk,kd->qrd/dot_general | solution.py:41
  313.0 4.2 %fusion.78 = bf16[8,256,4,128]{1,3,2,0:T(8,128)(2,1)} fusion(bf16[8,256,4,128]{1,3,2,0:T(8,128)(2,1)} %get-tuple-element.178, s32[]{:T(128)} %get-tuple-element.177, f32[4,256]{1,0:T(4,128)S(1)} %exponential_reduce_fusion.2, bf16[8,1280,128]{1,2,0:T(8,128)(2,1)} %get-tuple-element.190, pred[256,1280]{0,1:T(8,128)(4,1)S(1)} %compare_and_fusion.2, ...), kind=kOutput, calls=%fused_computation.10.clone.1 | convolution fusion | flops 677775616 | bytes 1513472 | tf_op jit(solution)/shard_map/while/body/eval_jaxpr/rqk,kd->qrd/dot_general | solution.py:41
  318.2 2.9 exponential_reduce_fusion.2
  321.1 4.2 %fusion.78 = bf16[8,256,4,128]{1,3,2,0:T(8,128)(2,1)} fusion(bf16[8,256,4,128]{1,3,2,0:T(8,128)(2,1)} %get-tuple-element.178, s32[]{:T(128)} %get-tuple-element.177, f32[4,256]{1,0:T(4,128)S(1)} %exponential_reduce_fusion.2, bf16[8,1280,128]{1,2,0:T(8,128)(2,1)} %get-tuple-element.190, pred[256,1280]{0,1:T(8,128)(4,1)S(1)} %compare_and_fusion.2, ...), kind=kOutput, calls=%fused_computation.10.clone.1 | convolution fusion | flops 677775616 | bytes 1513472 | tf_op jit(solution)/shard_map/while/body/eval_jaxpr/rqk,kd->qrd/dot_general | solution.py:41
  325.3 4.1 %copy.51 = bf16[1,256,4096]{2,1,0:T(8,128)(2,1)} copy(bf16[1,256,4096]{1,2,0:T(8,128)(2,1)} %bitcast.93) | data formatting | bytes 4194304 | tf_op jit(solution)/shard_map/reshape;reshape | solution.py:81
  (61 shorter events, 35.3 us)
Async XLA Ops:
  6.5 118.2 %copy-start = (bf16[1,256,5120]{2,1,0:T(8,128)(2,1)S(1)}, bf16[1,256,5120]{2,1,0:T(8,128)(2,1)}, u32[]{:S(2)}) copy-start(bf16[1,256,5120]{2,1,0:T(8,128)(2,1)} %param.8) | copy-start | bytes 7864324
  6.5 118.2 %copy-start.6 = (f32[5120]{0:T(1024)S(1)}, f32[5120]{0:T(1024)}, u32[]{:S(2)}) copy-start(f32[5120]{0:T(1024)} %param.10) | copy-start | bytes 61444
  6.5 118.2 %all-gather.2.cloned.1.call-start = ((), (), s32[]{:S(2)}) async-start(), calls=%async_computation | async-start | bytes 22282240 | tf_op jit(solution)/shard_map/all_gather | solution.py:58
  10.7 125.3 %copy-start.5 = (f32[1024]{0:T(1024)S(1)}, f32[1024]{0:T(1024)}, u32[]{:S(2)}) copy-start(f32[1024]{0:T(1024)} %param.12) | copy-start | bytes 12292
  134.6 1.3 copy-start.1
  136.0 10.8 %copy-start.2 = (f32[256,2048]{1,0:T(8,128)S(1)}, f32[256,2048]{1,0:T(8,128)}, u32[]{:S(2)}) copy-start(f32[256,2048]{1,0:T(8,128)} %copy-done.1) | copy-start | bytes 6291460
  136.3 17.8 %collective-permute-start = (bf16[256,8,128]{0,2,1:T(8,128)(2,1)S(1)}, bf16[256,8,128]{0,2,1:T(8,128)(2,1)}, u32[]{:S(2)}, u32[]{:S(2)}) collective-permute-start(bf16[256,8,128]{0,2,1:T(8,128)(2,1)S(1)} %bitcast.94), channel_id=1, source_target_pairs={{0,4},{1,5},{2,6},{3,7},{4,8},{5,9},{6,10},{7,11},{8,12},{9,13},{1... | collective-permute-start | bytes 1572872 | tf_op jit(solution)/shard_map/ppermute | solution.py:15
  137.7 54.5 %collective-permute-start.1 = (bf16[256,8,128]{0,2,1:T(8,128)(2,1)S(1)}, bf16[256,8,128]{0,2,1:T(8,128)(2,1)}, u32[]{:S(2)}, u32[]{:S(2)}) collective-permute-start(bf16[256,8,128]{0,2,1:T(8,128)(2,1)S(1)} %bitcast.95), channel_id=1, source_target_pairs={{0,3},{1,4},{2,5},{3,6},{4,7},{5,8},{6,9},{7,10},{8,11},{9,12},{10... | collective-permute-start | bytes 1572872 | tf_op jit(solution)/shard_map/ppermute | solution.py:15
  139.1 55.5 %collective-permute-start.2 = (bf16[256,8,128]{0,2,1:T(8,128)(2,1)S(1)}, bf16[256,8,128]{0,2,1:T(8,128)(2,1)}, u32[]{:S(2)}, u32[]{:S(2)}) collective-permute-start(bf16[256,8,128]{0,2,1:T(8,128)(2,1)S(1)} %bitcast.96), channel_id=1, source_target_pairs={{0,2},{1,3},{2,4},{3,5},{4,6},{5,7},{6,8},{7,9},{8,10},{9,11},{10,... | collective-permute-start | bytes 1572872 | tf_op jit(solution)/shard_map/ppermute | solution.py:15
  144.5 84.1 %collective-permute-start.3 = (bf16[256,8,128]{0,2,1:T(8,128)(2,1)S(1)}, bf16[256,8,128]{0,2,1:T(8,128)(2,1)S(1)}, u32[]{:S(2)}, u32[]{:S(2)}) collective-permute-start(bf16[256,8,128]{0,2,1:T(8,128)(2,1)S(1)} %bitcast.97), channel_id=1, source_target_pairs={{0,1},{1,2},{2,3},{3,4},{4,5},{5,6},{6,7},{7,8},{8,9},{9,10},{10,1... | collective-permute-start | bytes 1572872 | tf_op jit(solution)/shard_map/ppermute | solution.py:15
  147.0 81.8 %collective-permute-start.4 = (bf16[256,8,128]{2,0,1:T(8,128)(2,1)S(1)}, bf16[256,8,128]{2,0,1:T(8,128)(2,1)S(1)}, u32[]{:S(2)}, u32[]{:S(2)}) collective-permute-start(bf16[256,8,128]{2,0,1:T(8,128)(2,1)S(1)} %copy_bitcast_fusion), channel_id=1, source_target_pairs={{0,4},{1,5},{2,6},{3,7},{4,8},{5,9},{6,10},{7,11},{8,12},{9,13},{1... | collective-permute-start | bytes 1572872 | tf_op jit(solution)/shard_map/ppermute | solution.py:15
  154.0 74.7 %collective-permute-start.5 = (bf16[256,8,128]{2,0,1:T(8,128)(2,1)S(1)}, bf16[256,8,128]{2,0,1:T(8,128)(2,1)S(1)}, u32[]{:S(2)}, u32[]{:S(2)}) collective-permute-start(bf16[256,8,128]{2,0,1:T(8,128)(2,1)S(1)} %copy_bitcast_fusion), channel_id=1, source_target_pairs={{0,3},{1,4},{2,5},{3,6},{4,7},{5,8},{6,9},{7,10},{8,11},{9,12},{10... | collective-permute-start | bytes 1572872 | tf_op jit(solution)/shard_map/ppermute | solution.py:15
  192.3 42.8 %collective-permute-start.6 = (bf16[256,8,128]{2,0,1:T(8,128)(2,1)S(1)}, bf16[256,8,128]{2,0,1:T(8,128)(2,1)S(1)}, u32[]{:S(2)}, u32[]{:S(2)}) collective-permute-start(bf16[256,8,128]{2,0,1:T(8,128)(2,1)S(1)} %copy_bitcast_fusion), channel_id=1, source_target_pairs={{0,2},{1,3},{2,4},{3,5},{4,6},{5,7},{6,8},{7,9},{8,10},{9,11},{10,... | collective-permute-start | bytes 1572872 | tf_op jit(solution)/shard_map/ppermute | solution.py:15
  194.6 64.2 %collective-permute-start.7 = (bf16[256,8,128]{2,0,1:T(8,128)(2,1)S(1)}, bf16[256,8,128]{2,0,1:T(8,128)(2,1)S(1)}, u32[]{:S(2)}, u32[]{:S(2)}) collective-permute-start(bf16[256,8,128]{2,0,1:T(8,128)(2,1)S(1)} %copy_bitcast_fusion), channel_id=1, source_target_pairs={{0,1},{1,2},{2,3},{3,4},{4,5},{5,6},{6,7},{7,8},{8,9},{9,10},{10,1... | collective-permute-start | bytes 1572872 | tf_op jit(solution)/shard_map/ppermute | solution.py:15
  228.7 30.3 %copy-start.3 = (bf16[1280,8,128]{0,2,1:T(8,128)(2,1)}, bf16[1280,8,128]{0,2,1:T(8,128)(2,1)S(1)}, u32[]{:S(2)}) copy-start(bf16[1280,8,128]{0,2,1:T(8,128)(2,1)S(1)} %constant_dynamic-update-slice_fusion) | copy-start | bytes 7864324
  259.1 1.5 copy-start.4
Sparse Core Ops, SparseCore 0:
  9.2 115.4 all-gather.1
where the time goes:
time: 337 us; the launch traced here: 336 us
  waiting for transfers between devices  186 us (55%)
  matrix products  66.3 us (20%)
  starting transfers between devices  43.1 us (13%)
  local copies, waits for them, and re-layouts  15.8 us (5%)
  between operations  13.7 us (4%)
  other arithmetic  11 us (3%)
    all_gather x1, waiting for transfers between devices, shards(): lax.all_gather(kv_weight, 'fsdp', axis=0, tiled=True)  114 us
    ppermute x8, waiting for transfers between devices, from_behind(): return lax.ppermute(value, axis, pairs)  71.5 us
    ppermute x8, starting transfers between devices, from_behind(): return lax.ppermute(value, axis, pairs)  43.1 us
    dot_general x8, matrix products, one_group(): jnp.einsum('rqk,kd->qrd', probs, value_one, preferred_element_type=jnp.fl...  33.3 us
    sub x8, matrix products, one_group(): probs = jnp.exp(scores - highest)  23.1 us
    unnamed x23, local copies, waits for them, and re-layouts  10.5 us
    dot_general x1, matrix products, shards(): jnp.dot(normed, lax.all_gather(kv_weight, 'fsdp', axis=0, tiled=True), pr...  9.9 us
    and x8, other arithmetic, attend_near(): (key_pos[None, :] >= 0) & (key_pos[None, :] <= query_pos[:, None])  8.24 us
  transfers between devices with their start and end apart: 9, of which 5 were waited for; matrix products, arithmetic and copies ran while one was open for 3% of the time, Pallas kernels for 0%

commit v1 on v0

--- a/solution.py
+++ b/solution.py
@@ -55,7 +55,9 @@
     ).astype(jnp.bfloat16)
     projected = jnp.dot(
         normed,
-        lax.all_gather(kv_weight, "fsdp", axis=0, tiled=True),
+        jnp.concatenate(
+            lax.all_to_all(jnp.stack([kv_weight] * lax.axis_size("fsdp")), "fsdp", 0, 0), axis=0
+        ),
         preferred_element_type=jnp.float32,
     )
     keys = projected[:, : KVH * HD].astype(jnp.bfloat16).reshape(token_count, KVH, HD)

time: 337 us -> 450 us (1.34)
  waiting for transfers between devices: 186 us -> 277 us
  starting transfers between devices: 43.1 us -> 72.6 us
  between operations: 13.7 us -> 0.3 us
  local copies, waits for them, and re-layouts: 15.8 us -> 23.3 us
    all_to_all x0 -> x1, waiting for transfers between devices: none -> 228 us  [shards(): lax.all_to_all(jnp.stack([kv_weight] * lax.axis_size('fsdp')), 'fsdp', 0, 0)]
    all_gather x1 -> x0, waiting for transfers between devices: 114 us -> none  [shards(): lax.all_gather(kv_weight, 'fsdp', axis=0, tiled=True)]
    ppermute x8, starting transfers between devices: 43.1 us -> 66.6 us  [from_behind(): return lax.ppermute(value, axis, pairs)]
    ppermute x8, waiting for transfers between devices: 71.5 us -> 48.4 us  [from_behind(): return lax.ppermute(value, axis, pairs)]
    another operation x1 -> x2, local copies, waits for them, and re-layouts: 0.81 us -> 8.31 us  [the longest x1 8.23 us: shards(): jnp.stack([kv_weight] * lax.axis_size('fsdp'))]
    all_to_all x0 -> x1, starting transfers between devices: none -> 6 us  [shards(): lax.all_to_all(jnp.stack([kv_weight] * lax.axis_size('fsdp')), 'fsdp', 0, 0)]
    unnamed x23 -> x25, local copies, waits for them, and re-layouts: 10.5 us -> 10.5 us
  transfers between devices with their start and end apart: 9 -> 9, of which waited for: 5 -> 5; matrix products, arithmetic and copies ran while one was open for 3% -> 2% of each run, Pallas kernels for 0% -> 0%
where the time goes in v1:
time: 450 us; the launch traced here: 449 us
  waiting for transfers between devices  277 us (62%)
  starting transfers between devices  72.6 us (16%)
  matrix products  66.3 us (15%)
  local copies, waits for them, and re-layouts  23.3 us (5%)
  other arithmetic  9.31 us (2%)
    all_to_all x1, waiting for transfers between devices, shards(): lax.all_to_all(jnp.stack([kv_weight] * lax.axis_size('fsdp')), 'fsdp', 0, 0)  228 us
    ppermute x8, starting transfers between devices, from_behind(): return lax.ppermute(value, axis, pairs)  66.6 us
    ppermute x8, waiting for transfers between devices, from_behind(): return lax.ppermute(value, axis, pairs)  48.4 us
    dot_general x8, matrix products, one_group(): jnp.einsum('rqk,kd->qrd', probs, value_one, preferred_element_type=jnp.fl...  33.3 us
    sub x8, matrix products, one_group(): probs = jnp.exp(scores - highest)  23.1 us
    unnamed x25, local copies, waits for them, and re-layouts  10.5 us
    dot_general x1, matrix products, shards(): jnp.dot(normed, jnp.concatenate(lax.all_to_all(jnp.stack([kv_weight] * la...  9.91 us
  transfers between devices with their start and end apart: 9, of which 5 were waited for; matrix products, arithmetic and copies ran while one was open for 2% of the time, Pallas kernels for 0%

profile of v1, /device:TPU:135, one launch (start us, length us, event | category | flops | bytes accessed | tf_op | source)
XLA Modules:
  0.0 448.7 jit_solution(5534120897545802778)
XLA Ops:
  0.0 8.2 %stack.2 = bf16[16,320,2048]{2,1,0:T(8,128)(2,1)} broadcast(bf16[320,2048]{1,0:T(8,128)(2,1)} %param.11), dimensions={1,2} | broadcast | bytes 22282240 | tf_op jit(solution)/shard_map/stack | solution.py:59
  8.2 6.0 %all-to-all-start = ((bf16[16,320,2048]{2,1,0:T(8,128)(2,1)}), bf16[16,320,2048]{2,1,0:T(8,128)(2,1)}, u32[]{:S(2)}, u32[]{:S(2)}) async-start(bf16[16,320,2048]{2,1,0:T(8,128)(2,1)} %stack.2), calls=%async_computation | async-start | bytes 41943040 | tf_op jit(solution)/shard_map/all_to_all | solution.py:59
  15.2 228.4 %all-to-all-done = bf16[16,320,2048]{2,1,0:T(8,128)(2,1)} async-done(((bf16[16,320,2048]{2,1,0:T(8,128)(2,1)}), bf16[16,320,2048]{2,1,0:T(8,128)(2,1)}, u32[]{:S(2)}, u32[]{:S(2)}) %all-to-all-start) | async-done | bytes 20971552 | tf_op jit(solution)/shard_map/all_to_all | solution.py:59
  243.6 9.9 %fusion.54 = f32[256,2048]{1,0:T(8,128)S(1)} fusion(bf16[5120,2048]{1,0:T(8,128)(2,1)} %bitcast.1, bf16[1,256,5120]{2,1,0:T(8,128)(2,1)S(1)} %copy-done, f32[5120]{0:T(1024)S(1)} %copy-done.7, f32[256]{0:T(256)S(1)} %add_rsqrt_fusion), kind=kOutput, calls=%fused_computation.38 | convolution fusion | flops 5373952000 | bytes 25711616 | tf_op jit(solution)/shard_map/dot_general | solution.py:56
  259.3 4.1 copy.46
  263.4 3.1 collective-permute-start.3
  267.9 7.0 %collective-permute-done = bf16[256,8,128]{0,2,1:T(8,128)(2,1)} collective-permute-done((bf16[256,8,128]{0,2,1:T(8,128)(2,1)S(1)}, bf16[256,8,128]{0,2,1:T(8,128)(2,1)}, u32[]{:S(2)}, u32[]{:S(2)}) %collective-permute-start) | collective-permute-done | bytes 524320 | tf_op jit(solution)/shard_map/ppermute | solution.py:15
  277.3 11.4 %collective-permute-done.1 = bf16[256,8,128]{0,2,1:T(8,128)(2,1)} collective-permute-done((bf16[256,8,128]{0,2,1:T(8,128)(2,1)S(1)}, bf16[256,8,128]{0,2,1:T(8,128)(2,1)}, u32[]{:S(2)}, u32[]{:S(2)}) %collective-permute-start.1) | collective-permute-done | bytes 524320 | tf_op jit(solution)/shard_map/ppermute | solution.py:15
  291.1 55.7 %collective-permute-start.7 = (bf16[256,8,128]{2,0,1:T(8,128)(2,1)S(1)}, bf16[256,8,128]{2,0,1:T(8,128)(2,1)S(1)}, u32[]{:S(2)}, u32[]{:S(2)}) collective-permute-start(bf16[256,8,128]{2,0,1:T(8,128)(2,1)S(1)} %copy_bitcast_fusion), channel_id=1, source_target_pairs={{0,1},{1,2},{2,3},{3,4},{4,5},{5,6},{6,7},{7,8},{8,9},{9,10},{10,1... | collective-permute-start | bytes 1572872 | tf_op jit(solution)/shard_map/ppermute | solution.py:15
  348.2 5.5 %collective-permute-done.6 = bf16[256,8,128]{2,0,1:T(8,128)(2,1)S(1)} collective-permute-done((bf16[256,8,128]{2,0,1:T(8,128)(2,1)S(1)}, bf16[256,8,128]{2,0,1:T(8,128)(2,1)S(1)}, u32[]{:S(2)}, u32[]{:S(2)}) %collective-permute-start.6) | collective-permute-done | bytes 524320 | tf_op jit(solution)/shard_map/ppermute | solution.py:15
  353.7 24.4 %collective-permute-done.7 = bf16[256,8,128]{2,0,1:T(8,128)(2,1)S(1)} collective-permute-done((bf16[256,8,128]{2,0,1:T(8,128)(2,1)S(1)}, bf16[256,8,128]{2,0,1:T(8,128)(2,1)S(1)}, u32[]{:S(2)}, u32[]{:S(2)}) %collective-permute-start.7) | collective-permute-done | bytes 524320 | tf_op jit(solution)/shard_map/ppermute | solution.py:15
  379.9 64.7 %while.11 = (s32[]{:T(128)}, bf16[8,256,4,128]{1,3,2,0:T(8,128)(2,1)}, bf16[8,1280,128]{1,2,0:T(8,128)(2,1)}, bf16[8,1280,128]{2,1,0:T(8,128)(2,1)}, bf16[8,256,...) while((s32[]{:T(128)}, ...), condition=%wide.region_7.8_spmd.clone, body=%wide.region_4.7_spmd.clone.sunk | while | flops 1019874816 | bytes 2777453 | solution.py:44
  383.8 4.2 fusion.78
  391.9 4.1 fusion.78
  399.9 4.1 fusion.78
  408.0 4.2 fusion.78
  413.2 2.9 exponential_reduce_fusion.2
  416.1 4.2 fusion.78
  421.3 2.9 exponential_reduce_fusion.2
  424.2 4.2 fusion.78
  432.3 4.2 fusion.78
  437.5 2.9 exponential_reduce_fusion.2
  440.4 4.2 fusion.78
  444.6 4.1 copy.51
  (63 shorter events, 38.5 us)
Async XLA Ops:
  8.2 6.0 %copy-start.6 = (s32[1,16]{1,0:T(1,128)S(1)}, s32[1,16]{1,0:T(1,128)}, u32[]{:S(2)}) copy-start(s32[1,16]{1,0:T(1,128)} %param.13) | copy-start | bytes 196
  8.2 6.4 %copy-start = (bf16[1,256,5120]{2,1,0:T(8,128)(2,1)S(1)}, bf16[1,256,5120]{2,1,0:T(8,128)(2,1)}, u32[]{:S(2)}) copy-start(bf16[1,256,5120]{2,1,0:T(8,128)(2,1)} %param.8) | copy-start | bytes 7864324
  8.2 235.4 %all-to-all-start = ((bf16[16,320,2048]{2,1,0:T(8,128)(2,1)}), bf16[16,320,2048]{2,1,0:T(8,128)(2,1)}, u32[]{:S(2)}, u32[]{:S(2)}) async-start(bf16[16,320,2048]{2,1,0:T(8,128)(2,1)} %stack.2), calls=%async_computation | async-start | bytes 41943040 | tf_op jit(solution)/shard_map/all_to_all | solution.py:59
  14.2 229.4 %copy-start.7 = (f32[5120]{0:T(1024)S(1)}, f32[5120]{0:T(1024)}, u32[]{:S(2)}) copy-start(f32[5120]{0:T(1024)} %param.10) | copy-start | bytes 61444
  243.6 11.2 %copy-start.5 = (f32[1024]{0:T(1024)S(1)}, f32[1024]{0:T(1024)}, u32[]{:S(2)}) copy-start(f32[1024]{0:T(1024)} %param.12) | copy-start | bytes 12292
  253.5 1.3 copy-start.1
  255.0 11.6 %copy-start.2 = (f32[256,2048]{1,0:T(8,128)S(1)}, f32[256,2048]{1,0:T(8,128)}, u32[]{:S(2)}) copy-start(f32[256,2048]{1,0:T(8,128)} %copy-done.1) | copy-start | bytes 6291460
  255.2 19.7 %collective-permute-start = (bf16[256,8,128]{0,2,1:T(8,128)(2,1)S(1)}, bf16[256,8,128]{0,2,1:T(8,128)(2,1)}, u32[]{:S(2)}, u32[]{:S(2)}) collective-permute-start(bf16[256,8,128]{0,2,1:T(8,128)(2,1)S(1)} %bitcast.91), channel_id=1, source_target_pairs={{0,4},{1,5},{2,6},{3,7},{4,8},{5,9},{6,10},{7,11},{8,12},{9,13},{1... | collective-permute-start | bytes 1572872 | tf_op jit(solution)/shard_map/ppermute | solution.py:15
  256.6 32.1 %collective-permute-start.1 = (bf16[256,8,128]{0,2,1:T(8,128)(2,1)S(1)}, bf16[256,8,128]{0,2,1:T(8,128)(2,1)}, u32[]{:S(2)}, u32[]{:S(2)}) collective-permute-start(bf16[256,8,128]{0,2,1:T(8,128)(2,1)S(1)} %bitcast.92), channel_id=1, source_target_pairs={{0,3},{1,4},{2,5},{3,6},{4,7},{5,8},{6,9},{7,10},{8,11},{9,12},{10... | collective-permute-start | bytes 1572872 | tf_op jit(solution)/shard_map/ppermute | solution.py:15
  258.0 33.1 %collective-permute-start.2 = (bf16[256,8,128]{0,2,1:T(8,128)(2,1)S(1)}, bf16[256,8,128]{0,2,1:T(8,128)(2,1)}, u32[]{:S(2)}, u32[]{:S(2)}) collective-permute-start(bf16[256,8,128]{0,2,1:T(8,128)(2,1)S(1)} %bitcast.93), channel_id=1, source_target_pairs={{0,2},{1,3},{2,4},{3,5},{4,6},{5,7},{6,8},{7,9},{8,10},{9,11},{10,... | collective-permute-start | bytes 1572872 | tf_op jit(solution)/shard_map/ppermute | solution.py:15
  263.4 84.5 %collective-permute-start.3 = (bf16[256,8,128]{0,2,1:T(8,128)(2,1)S(1)}, bf16[256,8,128]{0,2,1:T(8,128)(2,1)S(1)}, u32[]{:S(2)}, u32[]{:S(2)}) collective-permute-start(bf16[256,8,128]{0,2,1:T(8,128)(2,1)S(1)} %bitcast.94), channel_id=1, source_target_pairs={{0,1},{1,2},{2,3},{3,4},{4,5},{5,6},{6,7},{7,8},{8,9},{9,10},{10,1... | collective-permute-start | bytes 1572872 | tf_op jit(solution)/shard_map/ppermute | solution.py:15
  266.6 81.4 %collective-permute-start.4 = (bf16[256,8,128]{2,0,1:T(8,128)(2,1)S(1)}, bf16[256,8,128]{2,0,1:T(8,128)(2,1)S(1)}, u32[]{:S(2)}, u32[]{:S(2)}) collective-permute-start(bf16[256,8,128]{2,0,1:T(8,128)(2,1)S(1)} %copy_bitcast_fusion), channel_id=1, source_target_pairs={{0,4},{1,5},{2,6},{3,7},{4,8},{5,9},{6,10},{7,11},{8,12},{9,13},{1... | collective-permute-start | bytes 1572872 | tf_op jit(solution)/shard_map/ppermute | solution.py:15
  274.9 73.1 %collective-permute-start.5 = (bf16[256,8,128]{2,0,1:T(8,128)(2,1)S(1)}, bf16[256,8,128]{2,0,1:T(8,128)(2,1)S(1)}, u32[]{:S(2)}, u32[]{:S(2)}) collective-permute-start(bf16[256,8,128]{2,0,1:T(8,128)(2,1)S(1)} %copy_bitcast_fusion), channel_id=1, source_target_pairs={{0,3},{1,4},{2,5},{3,6},{4,7},{5,8},{6,9},{7,10},{8,11},{9,12},{10... | collective-permute-start | bytes 1572872 | tf_op jit(solution)/shard_map/ppermute | solution.py:15
  288.7 64.9 %collective-permute-start.6 = (bf16[256,8,128]{2,0,1:T(8,128)(2,1)S(1)}, bf16[256,8,128]{2,0,1:T(8,128)(2,1)S(1)}, u32[]{:S(2)}, u32[]{:S(2)}) collective-permute-start(bf16[256,8,128]{2,0,1:T(8,128)(2,1)S(1)} %copy_bitcast_fusion), channel_id=1, source_target_pairs={{0,2},{1,3},{2,4},{3,5},{4,6},{5,7},{6,8},{7,9},{8,10},{9,11},{10,... | collective-permute-start | bytes 1572872 | tf_op jit(solution)/shard_map/ppermute | solution.py:15
  291.1 87.0 %collective-permute-start.7 = (bf16[256,8,128]{2,0,1:T(8,128)(2,1)S(1)}, bf16[256,8,128]{2,0,1:T(8,128)(2,1)S(1)}, u32[]{:S(2)}, u32[]{:S(2)}) collective-permute-start(bf16[256,8,128]{2,0,1:T(8,128)(2,1)S(1)} %copy_bitcast_fusion), channel_id=1, source_target_pairs={{0,1},{1,2},{2,3},{3,4},{4,5},{5,6},{6,7},{7,8},{8,9},{9,10},{10,1... | collective-permute-start | bytes 1572872 | tf_op jit(solution)/shard_map/ppermute | solution.py:15
  348.0 30.3 %copy-start.3 = (bf16[1280,8,128]{0,2,1:T(8,128)(2,1)}, bf16[1280,8,128]{0,2,1:T(8,128)(2,1)S(1)}, u32[]{:S(2)}) copy-start(bf16[1280,8,128]{0,2,1:T(8,128)(2,1)S(1)} %constant_dynamic-update-slice_fusion) | copy-start | bytes 7864324
  378.3 1.5 copy-start.4
